TPU v7x, 32 devices: a whole 2x2x4 slice. The times are simulated.
32 devices in a mesh: shard: 4 (over y, x), rep: 8 (over z, core).
Axes of the slice: x: 2, y: 2, z: 4, core: 2. Of those that a mesh axis runs over, the one named last changes fastest.
Arguments:
- activations: bfloat16 [8, 512, 2048], P('rep', 'shard'), may hold values from -16 to 16
- segments: int32 [8, 512], P('rep'), may hold values from 0 to 3, never falling along the last dimension, each value on 1 to 256 neighbouring positions
- attn_gain: float32 [2048], replicated, may hold values from 0.25 to 1.75
- query_weight: bfloat16 [2048, 2048], P('shard'), may hold values from -0.125 to 0.125
- key_weight: bfloat16 [2048, 1024], P('shard'), may hold values from -0.125 to 0.125
- value_weight: bfloat16 [2048, 1024], P('shard'), may hold values from -0.125 to 0.125
- query_gain: float32 [128], replicated, may hold values from 0.5 to 5.5
- key_gain: float32 [128], replicated, may hold values from 0.5 to 5.5
- out_weight: bfloat16 [2048, 2048], P('shard'), may hold values from -0.75 to 0.75
- mlp_gain: float32 [2048], replicated, may hold values from 0.25 to 1.75
- gate_weight: bfloat16 [2048, 6144], P('shard'), may hold values from -0.125 to 0.125
- up_weight: bfloat16 [2048, 6144], P('shard'), may hold values from -0.125 to 0.125
- down_weight: bfloat16 [6144, 2048], P('shard'), may hold values from -0.078125 to 0.078125
- cotangent: bfloat16 [8, 512, 2048], P('rep', 'shard'), may hold values from -11.1 to 11.1
Outputs:
- output: bfloat16 [8, 512, 2048], P('rep', 'shard')
- grad_input: float32 [8, 512, 2048], P('rep', 'shard')
- grad_attn_gain: float32 [2048], replicated
- grad_query_weight: float32 [2048, 2048], P('shard')
- grad_key_weight: float32 [2048, 1024], P('shard')
- grad_value_weight: float32 [2048, 1024], P('shard')
- grad_query_gain: float32 [128], replicated
- grad_key_gain: float32 [128], replicated
- grad_out_weight: float32 [2048, 2048], P('shard')
- grad_mlp_gain: float32 [2048], replicated
- grad_gate_weight: float32 [2048, 6144], P('shard')
- grad_up_weight: float32 [2048, 6144], P('shard')
- grad_down_weight: float32 [6144, 2048], P('shard')
Inputs may be any that keep to these rules, and one draw needn't show every extreme that they name: `segments`: within each sequence the document numbers never fall; each document has 1 to 256 tokens, and one has exactly 256.
All inputs are finite; a program needn't handle non-finite values.
Results may differ from a plain program's by a relative error of at most 0.02.
The roundings to bfloat16 on the way count: a program that leaves them out, or rounds other values in their place, can miss the bound.
Values may be sent and summed in bfloat16 or wider, within the bound.
A program may use at most 384 MiB of HBM per device.

v0:
```python
from functools import partial
import math
import jax
import jax.numpy as jnp
from jax import lax
from jax.sharding import PartitionSpec as P

HQ = 16
HK = 8
HD = 128
FF = 6144
EPSILON = 1e-06
ROPE_BASE = 1000000.0
MASKED = -1e30


def dims_last(left_op, right_op):
    return lax.dot_general(
        left_op, right_op, (((1,), (1,)), ((), ())), preferred_element_type=jnp.float32
    )


def dims_first(left_op, right_op):
    return lax.dot_general(
        left_op, right_op, (((0,), (0,)), ((), ())), preferred_element_type=jnp.float32
    )


def positions(seg_ids):
    token_index = jnp.arange(seg_ids.shape[0], dtype=jnp.int32)
    before = jnp.concatenate([jnp.full((1,), -1, jnp.int32), seg_ids[:-1]])
    starts = lax.cummax(
        jnp.where(seg_ids != before, token_index, jnp.zeros_like(token_index)), axis=0
    )
    return (token_index - starts).astype(jnp.float32)


def rotary(pos_float):
    half_width = HD // 2
    inv_freq = 1.0 / ROPE_BASE ** (jnp.arange(half_width, dtype=jnp.float32) * (2.0 / HD))
    angles = pos_float[:, None] * inv_freq[None, :]
    return (jnp.cos(angles), jnp.sin(angles))


def rotate(values_in, cosine, sine_part):
    half_width = values_in.shape[-1] // 2
    first_half = values_in[..., :half_width]
    second_half = values_in[..., half_width:]
    cos_b = cosine[:, None, :]
    sin_b = sine_part[:, None, :]
    return jnp.concatenate(
        [first_half * cos_b - second_half * sin_b, second_half * cos_b + first_half * sin_b], -1
    )


def rotate_back(grads_in, cosine, sine_part):
    half_width = grads_in.shape[-1] // 2
    first_half = grads_in[..., :half_width]
    second_half = grads_in[..., half_width:]
    cos_b = cosine[:, None, :]
    sin_b = sine_part[:, None, :]
    return jnp.concatenate(
        [first_half * cos_b + second_half * sin_b, second_half * cos_b - first_half * sin_b], -1
    )


def norm_back(grad_normed, values_in, rstat, gain_vec):
    scaled = values_in * rstat
    lead_axes = tuple(range(grad_normed.ndim - 1))
    grad_gain = jnp.sum(grad_normed * scaled, axis=lead_axes)
    weighted = grad_normed * gain_vec
    grad_values = rstat * (weighted - scaled * jnp.mean(weighted * scaled, -1, keepdims=True))
    return (grad_values, grad_gain)


def head_scores(query_group, key_block, visible, score_scale):
    scores = (
        jnp.einsum("qgd,kd->gqk", query_group, key_block, preferred_element_type=jnp.float32)
        * score_scale
    )
    return jnp.where(visible[None], scores, MASKED)


def attend(head_item, visible, score_scale):
    query_group, key_block, value_block = head_item
    scores = head_scores(query_group, key_block, visible, score_scale)
    row_max = jnp.max(scores, -1, keepdims=True)
    exp_scores = jnp.exp(scores - row_max)
    row_total = jnp.sum(exp_scores, -1, keepdims=True)
    softmax_out = (exp_scores / row_total).astype(jnp.bfloat16)
    head_out = jnp.einsum(
        "gqk,kd->qgd", softmax_out, value_block, preferred_element_type=jnp.float32
    )
    return (head_out, row_max + jnp.log(row_total))


def attend_back(head_item, visible, score_scale):
    query_group, key_block, value_block, grad_head, log_total = head_item
    scores = head_scores(query_group, key_block, visible, score_scale)
    softmax_out = jnp.exp(scores - log_total)
    grad_soft = jnp.einsum(
        "qgd,kd->gqk", grad_head, value_block, preferred_element_type=jnp.float32
    )
    row_delta = jnp.sum(softmax_out * grad_soft, -1, keepdims=True)
    grad_scores = (softmax_out * (grad_soft - row_delta)).astype(jnp.bfloat16)
    grad_group = (
        jnp.einsum("gqk,kd->qgd", grad_scores, key_block, preferred_element_type=jnp.float32)
        * score_scale
    )
    grad_key = (
        jnp.einsum("gqk,qgd->kd", grad_scores, query_group, preferred_element_type=jnp.float32)
        * score_scale
    )
    grad_value = jnp.einsum(
        "gqk,qgd->kd",
        softmax_out.astype(jnp.bfloat16),
        grad_head,
        preferred_element_type=jnp.float32,
    )
    return (grad_group, grad_key, grad_value)


def per_device(
    activations,
    segments,
    attn_gain,
    query_weight,
    key_weight,
    value_weight,
    query_gain,
    key_gain,
    out_weight,
    mlp_gain,
    gate_weight,
    up_weight,
    down_weight,
    cotangent,
):
    tok_rows = activations.shape[1]
    length = segments.shape[1]
    groups = HQ // HK
    score_scale = 1.0 / math.sqrt(HD)
    offset = lax.axis_index("shard") * tok_rows
    seg_ids = segments[0]
    pos_float = lax.dynamic_slice_in_dim(positions(seg_ids), offset, tok_rows)
    cosine, sine_part = rotary(pos_float)
    key_index = jnp.arange(length, dtype=jnp.int32)
    query_rows = offset + jnp.arange(tok_rows, dtype=jnp.int32)
    seg_rows = lax.dynamic_slice_in_dim(seg_ids, offset, tok_rows)
    visible = (key_index[None, :] <= query_rows[:, None]) & (seg_ids[None, :] == seg_rows[:, None])
    inputs = activations[0].astype(jnp.float32)
    rstat_attn = lax.rsqrt(jnp.mean(inputs * inputs, -1, keepdims=True) + EPSILON)
    normed = (inputs * rstat_attn * attn_gain).astype(jnp.bfloat16)
    full_query, full_key, full_value, full_out = (
        lax.all_gather(query_weight, "shard", axis=0, tiled=True),
        lax.all_gather(key_weight, "shard", axis=0, tiled=True),
        lax.all_gather(value_weight, "shard", axis=0, tiled=True),
        lax.all_gather(out_weight, "shard", axis=0, tiled=True),
    )
    queries = jnp.dot(normed, full_query, preferred_element_type=jnp.float32).reshape(
        tok_rows, HQ, HD
    )
    keys_raw = jnp.dot(normed, full_key, preferred_element_type=jnp.float32).reshape(
        tok_rows, HK, HD
    )
    values_low = jnp.dot(normed, full_value, preferred_element_type=jnp.float32).astype(
        jnp.bfloat16
    )
    query_rstat = lax.rsqrt(jnp.mean(queries * queries, -1, keepdims=True) + EPSILON)
    key_rstat = lax.rsqrt(jnp.mean(keys_raw * keys_raw, -1, keepdims=True) + EPSILON)
    query_rot = rotate(queries * query_rstat * query_gain, cosine, sine_part).astype(jnp.bfloat16)
    key_rot = rotate(keys_raw * key_rstat * key_gain, cosine, sine_part).astype(jnp.bfloat16)
    key_heads = jnp.transpose(key_rot, (1, 0, 2))
    value_heads = jnp.transpose(values_low.reshape(tok_rows, HK, HD), (1, 0, 2))
    all_keys, all_values = (
        lax.all_gather(key_heads, "shard", axis=1, tiled=True),
        lax.all_gather(value_heads, "shard", axis=1, tiled=True),
    )
    query_heads = jnp.transpose(query_rot.reshape(tok_rows, HK, groups, HD), (1, 0, 2, 3))
    attn_heads, log_totals = lax.map(
        partial(attend, visible=visible, score_scale=score_scale),
        (query_heads, all_keys, all_values),
    )
    attn_out = (
        jnp.transpose(attn_heads, (1, 0, 2, 3)).reshape(tok_rows, HQ * HD).astype(jnp.bfloat16)
    )
    hidden = inputs + jnp.dot(attn_out, full_out, preferred_element_type=jnp.float32)
    rstat_mlp = lax.rsqrt(jnp.mean(hidden * hidden, -1, keepdims=True) + EPSILON)
    normed_mlp = (hidden * rstat_mlp * mlp_gain).astype(jnp.bfloat16)
    full_gate, full_up, full_down = (
        lax.all_gather(gate_weight, "shard", axis=0, tiled=True),
        lax.all_gather(up_weight, "shard", axis=0, tiled=True),
        lax.all_gather(down_weight, "shard", axis=0, tiled=True),
    )
    gate_pre = jnp.dot(normed_mlp, full_gate, preferred_element_type=jnp.float32)
    up_pre = jnp.dot(normed_mlp, full_up, preferred_element_type=jnp.float32)
    sigmoid_gate = jax.nn.sigmoid(gate_pre)
    activated = (gate_pre * sigmoid_gate * up_pre).astype(jnp.bfloat16)
    result = hidden + jnp.dot(activated, full_down, preferred_element_type=jnp.float32)
    output = result.astype(jnp.bfloat16)[None]
    grad_out = cotangent[0]
    back_gate, back_up, back_down = (
        lax.all_gather(gate_weight, "shard", axis=0, tiled=True),
        lax.all_gather(up_weight, "shard", axis=0, tiled=True),
        lax.all_gather(down_weight, "shard", axis=0, tiled=True),
    )
    grad_act = dims_last(grad_out, back_down)
    grad_gate = (grad_act * up_pre * sigmoid_gate * (1.0 + gate_pre * (1.0 - sigmoid_gate))).astype(
        jnp.bfloat16
    )
    grad_up = (grad_act * gate_pre * sigmoid_gate).astype(jnp.bfloat16)
    grad_normed_mlp = dims_last(grad_gate, back_gate) + dims_last(grad_up, back_up)
    grad_hidden_part, grad_mlp_gain = norm_back(grad_normed_mlp, hidden, rstat_mlp, mlp_gain)
    grad_hidden = grad_out.astype(jnp.float32) + grad_hidden_part
    grad_branch = grad_hidden.astype(jnp.bfloat16)
    back_query, back_key, back_value, back_out = (
        lax.all_gather(query_weight, "shard", axis=0, tiled=True),
        lax.all_gather(key_weight, "shard", axis=0, tiled=True),
        lax.all_gather(value_weight, "shard", axis=0, tiled=True),
        lax.all_gather(out_weight, "shard", axis=0, tiled=True),
    )
    grad_attn = dims_last(grad_branch, back_out).astype(jnp.bfloat16)
    grad_heads = jnp.transpose(grad_attn.reshape(tok_rows, HK, groups, HD), (1, 0, 2, 3))
    grad_query_heads, grad_keys_all, grad_values_all = lax.map(
        partial(attend_back, visible=visible, score_scale=score_scale),
        (query_heads, all_keys, all_values, grad_heads, log_totals),
    )
    own_keys, own_values = (
        lax.psum_scatter(
            grad_keys_all.astype(jnp.bfloat16), "shard", scatter_dimension=1, tiled=True
        ).astype(jnp.float32),
        lax.psum_scatter(
            grad_values_all.astype(jnp.bfloat16), "shard", scatter_dimension=1, tiled=True
        ).astype(jnp.float32),
    )
    grad_query_rot = jnp.transpose(grad_query_heads, (1, 0, 2, 3)).reshape(tok_rows, HQ, HD)
    grad_key_rot = jnp.transpose(own_keys, (1, 0, 2))
    grad_value = (
        jnp.transpose(own_values, (1, 0, 2)).reshape(tok_rows, HK * HD).astype(jnp.bfloat16)
    )
    grad_query_norm, grad_query_gain = norm_back(
        rotate_back(grad_query_rot, cosine, sine_part), queries, query_rstat, query_gain
    )
    grad_key_norm, grad_key_gain = norm_back(
        rotate_back(grad_key_rot, cosine, sine_part), keys_raw, key_rstat, key_gain
    )
    grad_query = grad_query_norm.reshape(tok_rows, HQ * HD).astype(jnp.bfloat16)
    grad_key = grad_key_norm.reshape(tok_rows, HK * HD).astype(jnp.bfloat16)
    grad_normed = (
        dims_last(grad_query, back_query)
        + dims_last(grad_key, back_key)
        + dims_last(grad_value, back_value)
    )
    grad_input_part, grad_attn_gain = norm_back(grad_normed, inputs, rstat_attn, attn_gain)
    grad_input = (grad_hidden + grad_input_part)[None]
    grad_attn_gain, grad_query_gain, grad_key_gain, grad_mlp_gain = lax.psum(
        (grad_attn_gain, grad_query_gain, grad_key_gain, grad_mlp_gain), ("shard", "rep")
    )
    grad_qkv = jnp.concatenate([grad_query, grad_key, grad_value], 1)
    grad_mlp = jnp.concatenate([grad_gate, grad_up], 1)
    cols_attn, cols_mlp, cols_heads, cols_act = (
        lax.all_to_all(normed, "shard", split_axis=1, concat_axis=0, tiled=True),
        lax.all_to_all(normed_mlp, "shard", split_axis=1, concat_axis=0, tiled=True),
        lax.all_to_all(attn_out, "shard", split_axis=1, concat_axis=0, tiled=True),
        lax.all_to_all(activated, "shard", split_axis=1, concat_axis=0, tiled=True),
    )
    piece_qkv = lax.all_gather(grad_qkv, "shard", axis=0, tiled=True)
    piece_mlp = lax.all_gather(grad_mlp, "shard", axis=0, tiled=True)
    piece_branch = lax.all_gather(grad_branch, "shard", axis=0, tiled=True)
    piece_out = lax.all_gather(grad_out, "shard", axis=0, tiled=True)
    added_in = jnp.concatenate(
        [dims_first(cols_attn, piece_qkv), dims_first(cols_mlp, piece_mlp)], 1
    )
    part_out = dims_first(cols_heads, piece_branch)
    part_down = dims_first(cols_act, piece_out)
    owned_in, owned_out, owned_down = (
        lax.psum(added_in.astype(jnp.bfloat16), "rep").astype(jnp.float32),
        lax.psum(part_out.astype(jnp.bfloat16), "rep").astype(jnp.float32),
        lax.psum(part_down.astype(jnp.bfloat16), "rep").astype(jnp.float32),
    )
    width_query = HQ * HD
    width_kv = HK * HD
    edge_key = width_query + width_kv
    edge_value = edge_key + width_kv
    edge_gate = edge_value + FF
    grad_query_weight = owned_in[:, :width_query]
    grad_key_weight = owned_in[:, width_query:edge_key]
    grad_value_weight = owned_in[:, edge_key:edge_value]
    grad_gate_weight = owned_in[:, edge_value:edge_gate]
    grad_up_weight = owned_in[:, edge_gate:]
    return (
        output,
        grad_input,
        grad_attn_gain,
        grad_query_weight,
        grad_key_weight,
        grad_value_weight,
        grad_query_gain,
        grad_key_gain,
        owned_out,
        grad_mlp_gain,
        grad_gate_weight,
        grad_up_weight,
        owned_down,
    )


def solution(mesh):
    placed = (
        P("rep", "shard", None),
        P("rep", None),
        P(),
        P("shard", None),
        P("shard", None),
        P("shard", None),
        P(),
        P(),
        P("shard", None),
        P(),
        P("shard", None),
        P("shard", None),
        P("shard", None),
        P("rep", "shard", None),
    )
    return jax.shard_map(
        per_device,
        mesh=mesh,
        in_specs=placed,
        out_specs=(
            P("rep", "shard", None),
            P("rep", "shard", None),
            P(),
            P("shard", None),
            P("shard", None),
            P("shard", None),
            P(),
            P(),
            P("shard", None),
            P(),
            P("shard", None),
            P("shard", None),
            P("shard", None),
        ),
        check_vma=False,
    )
```

profile of v0, /device:TPU:0, one launch (start us, length us, event | category | flops | bytes accessed | tf_op | source)
XLA Modules:
  0.0 2083.6 jit_solution(7904533563809124515)
XLA Ops:
  11.7 53.4 %all-gather.19.cloned.1.call-done = bf16[2048,1024]{1,0:T(8,128)(2,1)} async-done(((bf16[512,1024]{1,0:T(8,128)(2,1)}), bf16[2048,1024]{1,0:T(8,128)(2,1)}) %all-gather.19.cloned.1.call-update) | async-done | bytes 4194320 | tf_op jit(solution)/shard_map/all_gather | solution.py:156
  65.2 6.5 copy.79
  71.7 3.7 multiply_reduce_fusion.9
  77.7 41.9 %all-gather.15.cloned.1.call-done = bf16[2048,1024]{1,0:T(8,128)(2,1)} async-done(((bf16[512,1024]{1,0:T(8,128)(2,1)}), bf16[2048,1024]{1,0:T(8,128)(2,1)}) %all-gather.15.cloned.1.call-update) | async-done | bytes 4194320 | tf_op jit(solution)/shard_map/all_gather | solution.py:157
  119.6 3.0 fusion.53
  128.3 20.1 all-gather.21.cloned.1.call-done
  150.0 87.6 %all-gather.23.cloned.1.call-done = bf16[2048,2048]{1,0:T(8,128)(2,1)} async-done(((bf16[512,2048]{1,0:T(8,128)(2,1)}), bf16[2048,2048]{1,0:T(8,128)(2,1)}) %all-gather.23.cloned.1.call-update) | async-done | bytes 8388624 | tf_op jit(solution)/shard_map/all_gather | solution.py:155
  237.6 12.2 copy.80
  249.9 5.8 multiply_reduce_fusion.6
  259.7 6.7 all-gather.17.cloned.1.call-done
  266.4 28.7 %while.30 = (s32[]{:T(128)}, bf16[8,128,2,128]{1,3,2,0:T(8,128)(2,1)}, f32[8,2,128,1]{2,1,3,0:T(2,128)}, bf16[8,512,128]{2,1,0:T(8,128)(2,1)}, bf16[8,512,128]{2...) while((s32[]{:T(128)}, ...), condition=%wide.region_8.9_spmd.clone.clone, body=%wide.region_5.8_spmd.clone.sunk.clone | while | flops 68353792 | bytes 2176605 | solution.py:180
  295.1 60.5 %all-gather.25.cloned.1.call-done = bf16[2048,2048]{1,0:T(8,128)(2,1)} async-done(((bf16[512,2048]{1,0:T(8,128)(2,1)}), bf16[2048,2048]{1,0:T(8,128)(2,1)}) %all-gather.25.cloned.1.call-update) | async-done | bytes 8388624 | tf_op jit(solution)/shard_map/all_gather | solution.py:158
  355.6 4.9 multiply_reduce_fusion.5
  360.8 224.3 %all-gather.27.cloned.1.call-done = bf16[2048,6144]{1,0:T(8,128)(2,1)} async-done(((bf16[512,6144]{1,0:T(8,128)(2,1)}), bf16[2048,6144]{1,0:T(8,128)(2,1)}) %all-gather.27.cloned.1.call-update) | async-done | bytes 25165840 | tf_op jit(solution)/shard_map/all_gather | solution.py:191
  585.1 13.7 fusion.86
  598.8 215.8 %all-gather.29.cloned.1.call-done = bf16[2048,6144]{1,0:T(8,128)(2,1)} async-done(((bf16[512,6144]{1,0:T(8,128)(2,1)}), bf16[2048,6144]{1,0:T(8,128)(2,1)}) %all-gather.29.cloned.1.call-update) | async-done | bytes 25165840 | tf_op jit(solution)/shard_map/all_gather | solution.py:192
  814.6 13.7 fusion.87
  828.3 215.8 %all-gather.31.cloned.1.call-done = bf16[6144,2048]{1,0:T(8,128)(2,1)} async-done(((bf16[1536,2048]{1,0:T(8,128)(2,1)}), bf16[6144,2048]{1,0:T(8,128)(2,1)}) %all-gather.31.cloned.1.call-update) | async-done | bytes 25165840 | tf_op jit(solution)/shard_map/all_gather | solution.py:193
  1044.1 16.8 multiply_convert_fusion.1
  1060.9 14.5 fusion.88
  1075.4 15.3 multiply_reduce_fusion.1
  1093.1 6.4 convolution_convert_fusion.4
  1102.7 86.9 %while.31 = (s32[]{:T(128)}, f32[8,128,2,128]{1,3,2,0:T(8,128)}, bf16[8,512,128]{1,2,0:T(8,128)(2,1)}, bf16[8,512,128]{1,2,0:T(8,128)(2,1)}, bf16[8,512,128]{2,1...) while((s32[]{:T(128)}, f32[8,128,2,128]{1,3,2,0:T(8,128)}, ...), condition=%wide.region_13.14_spmd.clone.clone, body=%wide.region_11.13_spmd.clone.sunk.clone | while | flops 169312000 | bytes 5780601 | solution.py:224
  1204.2 18.4 reduce-scatter.7.cloned.1.call-done
  1223.8 30.2 %reduce-scatter.9.cloned.1.call-done = bf16[128,1024]{1,0:T(8,128)(2,1)} async-done(((bf16[512,1024]{1,0:T(8,128)(2,1)}), bf16[128,1024]{1,0:T(8,128)(2,1)}) %reduce-scatter.9.cloned.1.call-update) | async-done | bytes 262160
  1256.8 3.8 pad_maximum_fusion.1
  1260.7 4.2 all-to-all-start.2
  1264.9 2.7 copy.136
  1267.6 9.6 all-to-all-done.2
  1277.3 4.4 all-to-all-start.3
  1288.6 23.6 %all-to-all-done.3 = bf16[128,4,1536]{2,0,1:T(8,128)(2,1)} async-done(((bf16[128,4,1536]{2,0,1:T(8,128)(2,1)}), bf16[128,4,1536]{2,0,1:T(8,128)(2,1)}, u32[]{:S(2)}, u32[]{:S(2)}) %all-to-all-start.3) | async-done | bytes 1572896 | tf_op jit(solution)/shard_map/all_to_all | solution.py:265
  1312.3 3.5 all-to-all-start
  1315.8 8.2 convolution_convert_fusion.1
  1324.0 25.4 %all-gather.37.cloned.1.call-done = bf16[512,2048]{1,0:T(8,128)(2,1)} async-done(((bf16[128,2048]{1,0:T(8,128)(2,1)}), bf16[512,2048]{1,0:T(8,128)(2,1)}) %all-gather.37.cloned.1.call-update) | async-done | bytes 2097168 | tf_op jit(solution)/shard_map/all_gather | solution.py:269
  1349.5 4.4 convolution_convert_fusion.3
  1354.6 3.5 all-to-all-start.1
  1358.2 49.5 %all-gather.33.cloned.1.call-done = bf16[512,4096]{0,1:T(8,128)(2,1)} async-done(((bf16[128,4096]{0,1:T(8,128)(2,1)}), bf16[512,4096]{0,1:T(8,128)(2,1)}) %all-gather.33.cloned.1.call-update) | async-done | bytes 4194320 | tf_op jit(solution)/shard_map/all_gather | solution.py:267
  1407.7 6.8 convolution_convert_fusion.2
  1414.5 117.9 %all-gather.35.cloned.1.call-done = bf16[512,12288]{1,0:T(8,128)(2,1)} async-done(((bf16[128,12288]{1,0:T(8,128)(2,1)}), bf16[512,12288]{1,0:T(8,128)(2,1)}) %all-gather.35.cloned.1.call-update) | async-done | bytes 12582928 | tf_op jit(solution)/shard_map/all_gather | solution.py:268
  1532.4 11.7 convolution_convert_fusion
  1544.1 9.0 pad_maximum_fusion
  1553.2 6.4 fusion.89
  1559.6 11.3 fusion.51
  1575.8 41.9 %all-reduce = (f32[2048]{0:T(1024)}, f32[128]{0:T(128)}, f32[128]{0:T(128)}, f32[2048]{0:T(1024)}) all-reduce(f32[2048]{0:T(1024)S(1)} %get-tuple-element.250, f32[128]{0:T(128)S(1)} %get-tuple-element.246, f32[128]{0:T(128)S(1)} %get-tuple-element.252, f32[2048]{0:T(1024)S(1)} %copy-done.29), channel_id=1, replica_groups=mesh['shard'=4,'rep'=8] {'shard','rep'}, use_global_device_ids=true, to_apply=%region_20.21 | all-reduce | flops 4352 | bytes 34816 | tf_op jit(solution)/shard_map/psum | solution.py:256
  1617.8 2.8 fusion.66
  1620.5 424.3 %all-reduce.4.cloned.1.call-done = (bf16[512,16384]{1,0:T(8,128)(2,1)}, bf16[512,2048]{1,0:T(8,128)(2,1)}, bf16[1536,2048]{1,0:T(8,128)(2,1)}) async-done(((bf16[512,16384]{1,0:T(8,128)(2,1)}, bf16[512,2048]{1,0:T(8,128)(2,1)}, bf16[1536,2048]{1,0:T(8,128)(2,1)}), (bf16[512,16384]{1,0:T(8,128)(2,1)}, bf16[512,2048]{1,0:T(8,128)(2,1)}, bf16[1536,2048]{1,0:T(8,128)(2,1)})) %all-reduce.4.cloned.1.call-update) | async-done | bytes 25165840 | tf_op jit(solution)/shard_map/psum | solution.py:277
  2044.9 15.6 fusion.84
  2068.0 6.3 convert_element_type.162
  (305 shorter events, 180.1 us)
Async XLA Ops:
  7.2 58.0 %all-gather.19.cloned.1.call-start = ((), (), s32[]{:S(2)}) async-start(), calls=%async_computation.8 | async-start | bytes 5242880 | tf_op jit(solution)/shard_map/all_gather | solution.py:156
  7.9 111.7 %all-gather.15.cloned.1.call-start = ((), (), s32[]{:S(2)}) async-start(), calls=%async_computation.6 | async-start | bytes 5242880 | tf_op jit(solution)/shard_map/all_gather | solution.py:157
  8.7 139.7 %all-gather.21.cloned.1.call-start = ((), (), s32[]{:S(2)}) async-start(), calls=%async_computation.9 | async-start | bytes 1310720 | tf_op jit(solution)/shard_map/all_gather | solution.py:176
  11.5 238.4 %copy-start.30 = (f32[128]{0:T(128)}, f32[128]{0:T(128)S(1)}, u32[]{:S(2)}) copy-start(f32[128]{0:T(128)S(1)} %add_rsqrt_fusion.3) | copy-start | bytes 1540
  11.7 244.3 %copy-start.18 = (f32[128,64]{0,1:T(8,128)}, f32[128,64]{0,1:T(8,128)S(1)}, u32[]{:S(2)}) copy-start(f32[128,64]{0,1:T(8,128)S(1)} %get-tuple-element.322) | copy-start | bytes 98308
  11.7 244.3 %copy-start.20 = (f32[128,64]{0,1:T(8,128)}, f32[128,64]{0,1:T(8,128)S(1)}, u32[]{:S(2)}) copy-start(f32[128,64]{0,1:T(8,128)S(1)} %get-tuple-element.323) | copy-start | bytes 98308
  65.2 6.5 copy-start.1
  65.2 6.5 copy-start.24
  77.1 160.5 %all-gather.23.cloned.1.call-start = ((), (), s32[]{:S(2)}) async-start(), calls=%async_computation.10 | async-start | bytes 10485760 | tf_op jit(solution)/shard_map/all_gather | solution.py:155
  77.7 188.7 %all-gather.17.cloned.1.call-start = ((), (), s32[]{:S(2)}) async-start(), calls=%async_computation.7 | async-start | bytes 1310720 | tf_op jit(solution)/shard_map/all_gather | solution.py:177
  123.3 232.3 %all-gather.25.cloned.1.call-start = ((), (), s32[]{:S(2)}) async-start(), calls=%async_computation.11 | async-start | bytes 10485760 | tf_op jit(solution)/shard_map/all_gather | solution.py:158
  123.9 461.2 %all-gather.27.cloned.1.call-start = ((), (), s32[]{:S(2)}) async-start(), calls=%async_computation.12 | async-start | bytes 31457280 | tf_op jit(solution)/shard_map/all_gather | solution.py:191
  124.7 689.9 %all-gather.29.cloned.1.call-start = ((), (), s32[]{:S(2)}) async-start(), calls=%async_computation.13 | async-start | bytes 31457280 | tf_op jit(solution)/shard_map/all_gather | solution.py:192
  125.4 918.6 %all-gather.31.cloned.1.call-start = ((), (), s32[]{:S(2)}) async-start(), calls=%async_computation.14 | async-start | bytes 31457280 | tf_op jit(solution)/shard_map/all_gather | solution.py:193
  126.2 1096.4 %reduce-scatter.7.cloned.1.call-start = ((), (), s32[]{:S(2)}) async-start(), calls=%async_computation.19 | async-start | bytes 1310720
  255.7 10.7 copy-start.27
  295.1 60.5 %copy-start.7 = (bf16[8,512,128]{2,1,0:T(8,128)(2,1)}, bf16[8,512,128]{2,1,0:T(8,128)(2,1)S(1)}, u32[]{:S(2)}) copy-start(bf16[8,512,128]{2,1,0:T(8,128)(2,1)S(1)} %get-tuple-element.616) | copy-start | bytes 3145732
  295.1 60.5 %copy-start.14 = (bf16[8,128,2,128]{3,1,2,0:T(8,128)(2,1)}, bf16[8,128,2,128]{3,1,2,0:T(8,128)(2,1)S(1)}, u32[]{:S(2)}) copy-start(bf16[8,128,2,128]{3,1,2,0:T(8,128)(2,1)S(1)} %get-tuple-element.632) | copy-start | bytes 1572868
  360.6 730.1 %copy-start.32 = (f32[128]{0:T(128)}, f32[128]{0:T(128)S(1)}, u32[]{:S(2)}) copy-start(f32[128]{0:T(128)S(1)} %add_rsqrt_fusion.2) | copy-start | bytes 1540
  360.8 453.8 %copy-start.4 = (bf16[128,2048]{1,0:T(8,128)(2,1)}, bf16[128,2048]{1,0:T(8,128)(2,1)S(1)}, u32[]{:S(2)}) copy-start(bf16[128,2048]{1,0:T(8,128)(2,1)S(1)} %multiply_convert_fusion.5) | copy-start | bytes 1572868
  1075.4 15.3 copy-start.11
  1090.7 8.8 copy-start.38
  1194.5 6.8 copy-start.19
  1194.5 6.8 copy-start.21
  1194.5 59.5 %reduce-scatter.9.cloned.1.call-start = ((), (), s32[]{:S(2)}) async-start(), calls=%async_computation.20 | async-start | bytes 1310720
  1194.5 8.1 copy-start.28
  1194.5 8.1 copy-start.37
  1199.5 116.3 %all-gather.39.cloned.1.call-start = ((), (), s32[]{:S(2)}) async-start(), calls=%async_computation.18 | async-start | bytes 2621440 | tf_op jit(solution)/shard_map/all_gather | solution.py:270
  1200.1 149.4 %all-gather.37.cloned.1.call-start = ((), (), s32[]{:S(2)}) async-start(), calls=%async_computation.17 | async-start | bytes 2621440 | tf_op jit(solution)/shard_map/all_gather | solution.py:269
  1200.8 206.9 %all-gather.33.cloned.1.call-start = ((), (), s32[]{:S(2)}) async-start(), calls=%async_computation.15 | async-start | bytes 5242880 | tf_op jit(solution)/shard_map/all_gather | solution.py:267
  1202.7 52.7 %copy-start.9 = (f32[128,8,128]{0,2,1:T(8,128)S(1)}, f32[128,8,128]{0,2,1:T(8,128)}, u32[]{:S(2)}) copy-start(f32[128,8,128]{0,2,1:T(8,128)} %copy-done.8) | copy-start | bytes 1572868
  1202.7 52.7 %copy-start.35 = (f32[128]{0:T(128)S(1)}, f32[128]{0:T(128)}, u32[]{:S(2)}) copy-start(f32[128]{0:T(128)} %param.25) | copy-start | bytes 1540
  1204.2 51.5 %copy-start.13 = (bf16[128,16,128]{0,2,1:T(8,128)(2,1)S(1)}, bf16[128,16,128]{0,2,1:T(8,128)(2,1)}, u32[]{:S(2)}) copy-start(bf16[128,16,128]{0,2,1:T(8,128)(2,1)} %multiply_convert_fusion.4) | copy-start | bytes 1572868
  1256.8 275.6 %all-gather.35.cloned.1.call-start = ((), (), s32[]{:S(2)}) async-start(), calls=%async_computation.16 | async-start | bytes 15728640 | tf_op jit(solution)/shard_map/all_gather | solution.py:268
  1260.7 16.6 all-to-all-start.2
  1264.9 18.5 copy-start.31
  1264.9 20.9 %copy-start.5 = (bf16[128,2048]{1,0:T(8,128)(2,1)S(1)}, bf16[128,2048]{1,0:T(8,128)(2,1)}, u32[]{:S(2)}) copy-start(bf16[128,2048]{1,0:T(8,128)(2,1)} %copy-done.4) | copy-start | bytes 1572868
  1277.3 35.0 %all-to-all-start.3 = ((bf16[128,4,1536]{2,0,1:T(8,128)(2,1)}), bf16[128,4,1536]{2,0,1:T(8,128)(2,1)}, u32[]{:S(2)}, u32[]{:S(2)}) async-start(bf16[128,4,1536]{2,0,1:T(8,128)(2,1)} %bitcast.331), calls=%async_computation.3 | async-start | bytes 3145728 | tf_op jit(solution)/shard_map/all_to_all | solution.py:265
  1312.3 41.6 %all-to-all-start = ((bf16[128,4,512]{2,0,1:T(8,128)(2,1)}), bf16[128,4,512]{2,0,1:T(8,128)(2,1)S(1)}, u32[]{:S(2)}, u32[]{:S(2)}) async-start(bf16[128,4,512]{2,0,1:T(8,128)(2,1)} %fusion.56), calls=%async_computation | async-start | bytes 1048576 | tf_op jit(solution)/shard_map/all_to_all | solution.py:262
  1354.6 59.8 %all-to-all-start.1 = ((bf16[128,4,512]{2,0,1:T(8,128)(2,1)}), bf16[128,4,512]{2,0,1:T(8,128)(2,1)S(1)}, u32[]{:S(2)}, u32[]{:S(2)}) async-start(bf16[128,4,512]{2,0,1:T(8,128)(2,1)} %bitcast.345), calls=%async_computation.1 | async-start | bytes 1048576 | tf_op jit(solution)/shard_map/all_to_all | solution.py:263
  1358.1 686.8 %all-reduce.4.cloned.1.call-start = ((), (), s32[]{:S(2)}) async-start(), calls=%async_computation.21 | async-start | bytes 50331648 | tf_op jit(solution)/shard_map/psum | solution.py:277
  1559.6 11.3 copy-start.3
  1573.1 44.6 %copy-start.6 = (f32[128,2048]{1,0:T(8,128)S(1)}, f32[128,2048]{1,0:T(8,128)}, u32[]{:S(2)}) copy-start(f32[128,2048]{1,0:T(8,128)} %get-tuple-element.330) | copy-start | bytes 3145732
  1573.1 44.6 %copy-start.12 = (bf16[1,128,2048]{2,1,0:T(8,128)(2,1)S(1)}, bf16[1,128,2048]{2,1,0:T(8,128)(2,1)}, u32[]{:S(2)}) copy-start(bf16[1,128,2048]{2,1,0:T(8,128)(2,1)} %param.31) | copy-start | bytes 1572868
  1573.1 44.6 %copy-start.26 = (f32[2048]{0:T(1024)S(1)}, f32[2048]{0:T(1024)}, u32[]{:S(2)}) copy-start(f32[2048]{0:T(1024)} %param.27) | copy-start | bytes 24580
  1573.1 44.6 %copy-start.33 = (f32[128]{0:T(128)S(1)}, f32[128]{0:T(128)}, u32[]{:S(2)}) copy-start(f32[128]{0:T(128)} %copy-done.32) | copy-start | bytes 1540
  1573.1 44.6 %copy-start.39 = (f32[128]{0:T(128)S(1)}, f32[128]{0:T(128)}, u32[]{:S(2)}) copy-start(f32[128]{0:T(128)} %copy-done.38) | copy-start | bytes 1540
  2044.9 18.0 copy-start
  (14 other events, 50.9 us)
Sparse Core Ops, SparseCore 0:
  9.8 55.2 all-gather.18
  67.0 52.5 all-gather.14
  122.0 26.3 all-gather.20
  150.1 87.4 all-gather.22
  239.9 26.4 all-gather.16
  268.1 87.4 all-gather.24
  357.5 227.5 all-gather.26
  587.0 227.5 all-gather.28
  816.4 227.5 all-gather.30
  1194.6 27.9 reduce-scatter.6
  1226.0 27.9 reduce-scatter.8
  1255.7 56.7 all-gather.38
  1314.3 35.1 all-gather.36
  1351.7 55.9 all-gather.32
  1410.0 122.3 all-gather.34
  1553.3 491.5 all-reduce.3
where the time goes:
time: 2090 us; the launch traced here: 2080 us
  waiting for transfers between devices  1630 us (78%)
  matrix products  228 us (11%)
  local copies, waits for them, and re-layouts  91.2 us (4%)
  other arithmetic  59.5 us (3%)
  blocking collectives  41.9 us (2%)
    psum x1, waiting for transfers between devices, per_device(): lax.psum(added_in.astype(jnp.bfloat16), 'rep').astype(jnp.float32)  424 us
    all_gather x1, waiting for transfers between devices, per_device(): lax.all_gather(gate_weight, 'shard', axis=0, tiled=True)  224 us
    all_gather x1, waiting for transfers between devices, per_device(): lax.all_gather(down_weight, 'shard', axis=0, tiled=True)  216 us
    all_gather x1, waiting for transfers between devices, per_device(): lax.all_gather(up_weight, 'shard', axis=0, tiled=True)  216 us
    all_gather x1, waiting for transfers between devices, per_device(): piece_mlp = lax.all_gather(grad_mlp, 'shard', axis=0, tiled=True)  118 us
    all_gather x1, waiting for transfers between devices, per_device(): lax.all_gather(query_weight, 'shard', axis=0, tiled=True)  87.6 us
    dot_general x7, matrix products, dims_last(): lax.dot_general(left_op, right_op, (((1,), (1,)), ((), ())), preferred_el...  63.7 us
    all_gather x1, waiting for transfers between devices, per_device(): lax.all_gather(out_weight, 'shard', axis=0, tiled=True)  60.5 us
  transfers between devices with their start and end apart: 20, of which 17 were waited for; matrix products, arithmetic and copies ran while one was open for 8% of the time, Pallas kernels for 0%

commit v1 on v0

--- a/solution.py
+++ b/solution.py
@@ -12,6 +12,18 @@
 EPSILON = 1e-06
 ROPE_BASE = 1000000.0
 MASKED = -1e30
+
+
+def collect(x, axis, dim):
+    ways, here, step = (lax.axis_size(axis), lax.axis_index(axis), x.shape[dim])
+    line, have = (x, 1)
+    while have < ways:
+        line = jnp.concatenate(
+            [line, lax.ppermute(line, axis, [(d, (d - have) % ways) for d in range(ways)])],
+            axis=dim,
+        )
+        have = 2 * have
+    return jnp.roll(line, here * step, axis=dim)
 
 
 def dims_last(left_op, right_op):
@@ -189,7 +201,7 @@
     normed_mlp = (hidden * rstat_mlp * mlp_gain).astype(jnp.bfloat16)
     full_gate, full_up, full_down = (
         lax.all_gather(gate_weight, "shard", axis=0, tiled=True),
-        lax.all_gather(up_weight, "shard", axis=0, tiled=True),
+        collect(up_weight, "shard", 0),
         lax.all_gather(down_weight, "shard", axis=0, tiled=True),
     )
     gate_pre = jnp.dot(normed_mlp, full_gate, preferred_element_type=jnp.float32)

time: 2090 us -> 2380 us (1.14)
  waiting for transfers between devices: 1630 us -> 1860 us
  local copies, waits for them, and re-layouts: 91.2 us -> 129 us
    ppermute x0 -> x2, waiting for transfers between devices: none -> 234 us  [collect(): lax.ppermute(line, axis, [(d, (d - have) % ways) for d in range(ways)])]
    all_gather x1, waiting for transfers between devices: 216 us -> 137 us  [per_device(): lax.all_gather(down_weight, 'shard', axis=0, tiled=True)]
    all_gather x1, waiting for transfers between devices: 60.5 us -> 128 us  [per_device(): lax.all_gather(out_weight, 'shard', axis=0, tiled=True)]
    all_gather x1, waiting for transfers between devices: 87.6 us -> 149 us  [per_device(): lax.all_gather(query_weight, 'shard', axis=0, tiled=True)]
    all_gather x1, waiting for transfers between devices: 216 us -> 183 us  [per_device(): lax.all_gather(up_weight, 'shard', axis=0, tiled=True)]
    unnamed x93 -> x108, local copies, waits for them, and re-layouts: 18.8 us -> 48 us
  transfers between devices with their start and end apart: 20 -> 22, of which waited for: 17 -> 18; matrix products, arithmetic and copies ran while one was open for 8% -> 11% of each run, Pallas kernels for 0% -> 0%
where the time goes in v1:
time: 2380 us; the launch traced here: 2370 us
  waiting for transfers between devices  1860 us (78%)
  matrix products  231 us (10%)
  local copies, waits for them, and re-layouts  129 us (5%)
  other arithmetic  70.5 us (3%)
  blocking collectives  41.9 us (2%)
    psum x1, waiting for transfers between devices, per_device(): lax.psum(added_in.astype(jnp.bfloat16), 'rep').astype(jnp.float32)  424 us
    ppermute x2, waiting for transfers between devices, collect(): lax.ppermute(line, axis, [(d, (d - have) % ways) for d in range(ways)])  234 us
    all_gather x1, waiting for transfers between devices, per_device(): lax.all_gather(gate_weight, 'shard', axis=0, tiled=True)  214 us
    all_gather x1, waiting for transfers between devices, per_device(): lax.all_gather(up_weight, 'shard', axis=0, tiled=True)  183 us
    all_gather x1, waiting for transfers between devices, per_device(): lax.all_gather(query_weight, 'shard', axis=0, tiled=True)  149 us
    all_gather x1, waiting for transfers between devices, per_device(): lax.all_gather(down_weight, 'shard', axis=0, tiled=True)  137 us
    all_gather x1, waiting for transfers between devices, per_device(): lax.all_gather(out_weight, 'shard', axis=0, tiled=True)  128 us
    all_gather x1, waiting for transfers between devices, per_device(): piece_mlp = lax.all_gather(grad_mlp, 'shard', axis=0, tiled=True)  118 us
  transfers between devices with their start and end apart: 22, of which 18 were waited for; matrix products, arithmetic and copies ran while one was open for 11% of the time, Pallas kernels for 0%

profile of v1, /device:TPU:0, one launch (start us, length us, event | category | flops | bytes accessed | tf_op | source)
XLA Modules:
  0.0 2370.0 jit_solution(1633411157119126199)
XLA Ops:
  11.7 53.4 %all-gather.19.cloned.1.call-done = bf16[2048,1024]{1,0:T(8,128)(2,1)} async-done(((bf16[512,1024]{1,0:T(8,128)(2,1)}), bf16[2048,1024]{1,0:T(8,128)(2,1)}) %all-gather.19.cloned.1.call-update) | async-done | bytes 4194320 | tf_op jit(solution)/shard_map/all_gather | solution.py:168
  65.2 6.4 copy.79
  71.6 3.7 multiply_reduce_fusion.9
  77.7 41.9 %all-gather.15.cloned.1.call-done = bf16[2048,1024]{1,0:T(8,128)(2,1)} async-done(((bf16[512,1024]{1,0:T(8,128)(2,1)}), bf16[2048,1024]{1,0:T(8,128)(2,1)}) %all-gather.15.cloned.1.call-update) | async-done | bytes 4194320 | tf_op jit(solution)/shard_map/all_gather | solution.py:169
  130.0 136.7 %collective-permute-done = bf16[512,6144]{1,0:T(8,128)(2,1)} collective-permute-done((bf16[512,6144]{1,0:T(8,128)(2,1)}, bf16[512,6144]{1,0:T(8,128)(2,1)}, u32[]{:S(2)}, u32[]{:S(2)}) %collective-permute-start) | collective-permute-done | bytes 6291488 | tf_op jit(solution)/shard_map/ppermute | solution.py:22
  266.7 10.4 pad_maximum_fusion.1
  281.6 6.2 constant_dynamic-update-slice_fusion.6
  289.5 148.8 %all-gather.23.cloned.1.call-done = bf16[2048,2048]{1,0:T(8,128)(2,1)} async-done(((bf16[512,2048]{1,0:T(8,128)(2,1)}), bf16[2048,2048]{1,0:T(8,128)(2,1)}) %all-gather.23.cloned.1.call-update) | async-done | bytes 8388624 | tf_op jit(solution)/shard_map/all_gather | solution.py:167
  438.3 12.2 copy.80
  450.6 5.8 multiply_reduce_fusion.6
  460.4 15.4 all-gather.17.cloned.1.call-done
  475.7 28.5 %while.30 = (s32[]{:T(128)}, bf16[8,128,2,128]{1,3,2,0:T(8,128)(2,1)}, f32[8,2,128,1]{2,1,3,0:T(2,128)}, bf16[8,512,128]{2,1,0:T(8,128)(2,1)}, bf16[8,512,128]{2...) while((s32[]{:T(128)}, ...), condition=%wide.region_8.9_spmd.clone.clone, body=%wide.region_5.8_spmd.clone.sunk.clone | while | flops 68353792 | bytes 2176605 | solution.py:192
  504.2 128.4 %all-gather.25.cloned.1.call-done = bf16[2048,2048]{1,0:T(8,128)(2,1)} async-done(((bf16[512,2048]{1,0:T(8,128)(2,1)}), bf16[2048,2048]{1,0:T(8,128)(2,1)}) %all-gather.25.cloned.1.call-update) | async-done | bytes 8388624 | tf_op jit(solution)/shard_map/all_gather | solution.py:170
  632.6 4.9 multiply_reduce_fusion.5
  638.5 97.4 %collective-permute-done.1 = bf16[1024,6144]{1,0:T(8,128)(2,1)} collective-permute-done((bf16[1024,6144]{1,0:T(8,128)(2,1)}, bf16[1024,6144]{1,0:T(8,128)(2,1)}, u32[]{:S(2)}, u32[]{:S(2)}) %collective-permute-start.1) | collective-permute-done | bytes 12582944 | tf_op jit(solution)/shard_map/ppermute | solution.py:22
  735.9 10.7 constant_dynamic-update-slice_fusion.5
  749.7 6.3 constant_dynamic-update-slice_fusion.3
  756.0 10.8 constant_dynamic-update-slice_fusion.2
  766.7 136.9 %all-gather.29.cloned.1.call-done = bf16[6144,2048]{1,0:T(8,128)(2,1)} async-done(((bf16[1536,2048]{1,0:T(8,128)(2,1)}), bf16[6144,2048]{1,0:T(8,128)(2,1)}) %all-gather.29.cloned.1.call-update) | async-done | bytes 25165840 | tf_op jit(solution)/shard_map/all_gather | solution.py:205
  903.6 15.2 fusion.74
  918.9 214.2 %all-gather.27.cloned.1.call-done = bf16[2048,6144]{1,0:T(8,128)(2,1)} async-done(((bf16[512,6144]{1,0:T(8,128)(2,1)}), bf16[2048,6144]{1,0:T(8,128)(2,1)}) %all-gather.27.cloned.1.call-update) | async-done | bytes 25165840 | tf_op jit(solution)/shard_map/all_gather | solution.py:203
  1133.1 13.9 fusion.89
  1147.0 18.0 multiply_convert_fusion.1
  1165.0 14.3 fusion.90
  1179.3 183.3 %all-gather.31.cloned.1.call-done = bf16[2048,6144]{1,0:T(8,128)(2,1)} async-done(((bf16[512,6144]{1,0:T(8,128)(2,1)}), bf16[2048,6144]{1,0:T(8,128)(2,1)}) %all-gather.31.cloned.1.call-update) | async-done | bytes 25165840 | tf_op jit(solution)/shard_map/all_gather | solution.py:216
  1362.6 15.6 multiply_reduce_fusion.1
  1380.6 6.4 convolution_convert_fusion.4
  1390.2 86.7 %while.31 = (s32[]{:T(128)}, f32[8,128,2,128]{1,3,2,0:T(8,128)}, bf16[8,512,128]{1,2,0:T(8,128)(2,1)}, bf16[8,512,128]{1,2,0:T(8,128)(2,1)}, bf16[8,512,128]{2,1...) while((s32[]{:T(128)}, f32[8,128,2,128]{1,3,2,0:T(8,128)}, ...), condition=%wide.region_13.14_spmd.clone.clone, body=%wide.region_11.13_spmd.clone.sunk.clone | while | flops 169312000 | bytes 5780601 | solution.py:236
  1491.1 18.8 reduce-scatter.7.cloned.1.call-done
  1511.2 30.2 %reduce-scatter.9.cloned.1.call-done = bf16[128,1024]{1,0:T(8,128)(2,1)} async-done(((bf16[512,1024]{1,0:T(8,128)(2,1)}), bf16[128,1024]{1,0:T(8,128)(2,1)}) %reduce-scatter.9.cloned.1.call-update) | async-done | bytes 262160
  1544.9 3.8 pad_maximum_fusion.2
  1555.1 9.4 all-to-all-done.2
  1564.5 4.4 all-to-all-start.3
  1574.0 25.6 %all-to-all-done.3 = bf16[128,4,1536]{2,0,1:T(8,128)(2,1)} async-done(((bf16[128,4,1536]{2,0,1:T(8,128)(2,1)}), bf16[128,4,1536]{2,0,1:T(8,128)(2,1)}, u32[]{:S(2)}, u32[]{:S(2)}) %all-to-all-start.3) | async-done | bytes 1572896 | tf_op jit(solution)/shard_map/all_to_all | solution.py:277
  1603.3 8.2 convolution_convert_fusion.1
  1611.6 25.3 %all-gather.37.cloned.1.call-done = bf16[512,2048]{1,0:T(8,128)(2,1)} async-done(((bf16[128,2048]{1,0:T(8,128)(2,1)}), bf16[512,2048]{1,0:T(8,128)(2,1)}) %all-gather.37.cloned.1.call-update) | async-done | bytes 2097168 | tf_op jit(solution)/shard_map/all_gather | solution.py:281
  1636.9 4.2 convolution_convert_fusion.3
  1644.6 49.5 %all-gather.33.cloned.1.call-done = bf16[512,4096]{0,1:T(8,128)(2,1)} async-done(((bf16[128,4096]{0,1:T(8,128)(2,1)}), bf16[512,4096]{0,1:T(8,128)(2,1)}) %all-gather.33.cloned.1.call-update) | async-done | bytes 4194320 | tf_op jit(solution)/shard_map/all_gather | solution.py:279
  1694.1 6.6 convolution_convert_fusion.2
  1700.7 118.1 %all-gather.35.cloned.1.call-done = bf16[512,12288]{1,0:T(8,128)(2,1)} async-done(((bf16[128,12288]{1,0:T(8,128)(2,1)}), bf16[512,12288]{1,0:T(8,128)(2,1)}) %all-gather.35.cloned.1.call-update) | async-done | bytes 12582928 | tf_op jit(solution)/shard_map/all_gather | solution.py:280
  1818.8 11.7 convolution_convert_fusion
  1830.5 8.9 pad_maximum_fusion
  1839.5 6.4 fusion.91
  1845.9 11.3 fusion.53
  1862.1 41.9 %all-reduce = (f32[2048]{0:T(1024)}, f32[128]{0:T(128)}, f32[128]{0:T(128)}, f32[2048]{0:T(1024)}) all-reduce(f32[2048]{0:T(1024)S(1)} %get-tuple-element.250, f32[128]{0:T(128)S(1)} %get-tuple-element.246, f32[128]{0:T(128)S(1)} %get-tuple-element.252, f32[2048]{0:T(1024)S(1)} %copy-done.30), channel_id=1, replica_groups=mesh['shard'=4,'rep'=8] {'shard','rep'}, use_global_device_ids=true, to_apply=%region_20.21 | all-reduce | flops 4352 | bytes 34816 | tf_op jit(solution)/shard_map/psum | solution.py:268
  1906.9 424.3 %all-reduce.4.cloned.1.call-done = (bf16[512,16384]{1,0:T(8,128)(2,1)}, bf16[512,2048]{1,0:T(8,128)(2,1)}, bf16[1536,2048]{1,0:T(8,128)(2,1)}) async-done(((bf16[512,16384]{1,0:T(8,128)(2,1)}, bf16[512,2048]{1,0:T(8,128)(2,1)}, bf16[1536,2048]{1,0:T(8,128)(2,1)}), (bf16[512,16384]{1,0:T(8,128)(2,1)}, bf16[512,2048]{1,0:T(8,128)(2,1)}, bf16[1536,2048]{1,0:T(8,128)(2,1)})) %all-reduce.4.cloned.1.call-update) | async-done | bytes 25165840 | tf_op jit(solution)/shard_map/psum | solution.py:289
  2331.2 15.6 fusion.87
  2354.4 6.3 convert_element_type.162
  (328 shorter events, 206.8 us)
Async XLA Ops:
  7.2 64.4 %copy-start.1 = (bf16[1,128,2048]{2,1,0:T(8,128)(2,1)S(1)}, bf16[1,128,2048]{2,1,0:T(8,128)(2,1)}, u32[]{:S(2)}) copy-start(bf16[1,128,2048]{2,1,0:T(8,128)(2,1)} %param.18) | copy-start | bytes 1572868
  7.2 64.4 %copy-start.25 = (f32[2048]{0:T(1024)S(1)}, f32[2048]{0:T(1024)}, u32[]{:S(2)}) copy-start(f32[2048]{0:T(1024)} %param.20) | copy-start | bytes 24580
  7.2 58.0 %all-gather.19.cloned.1.call-start = ((), (), s32[]{:S(2)}) async-start(), calls=%async_computation.8 | async-start | bytes 5242880 | tf_op jit(solution)/shard_map/all_gather | solution.py:168
  7.9 111.7 %all-gather.15.cloned.1.call-start = ((), (), s32[]{:S(2)}) async-start(), calls=%async_computation.6 | async-start | bytes 5242880 | tf_op jit(solution)/shard_map/all_gather | solution.py:169
  8.7 279.2 %all-gather.21.cloned.1.call-start = ((), (), s32[]{:S(2)}) async-start(), calls=%async_computation.9 | async-start | bytes 1310720 | tf_op jit(solution)/shard_map/all_gather | solution.py:188
  11.5 439.0 %copy-start.31 = (f32[128]{0:T(128)}, f32[128]{0:T(128)S(1)}, u32[]{:S(2)}) copy-start(f32[128]{0:T(128)S(1)} %add_rsqrt_fusion.3) | copy-start | bytes 1540
  11.7 444.9 %copy-start.20 = (f32[128,64]{0,1:T(8,128)}, f32[128,64]{0,1:T(8,128)S(1)}, u32[]{:S(2)}) copy-start(f32[128,64]{0,1:T(8,128)S(1)} %get-tuple-element.322) | copy-start | bytes 98308
  11.7 444.9 %copy-start.22 = (f32[128,64]{0,1:T(8,128)}, f32[128,64]{0,1:T(8,128)S(1)}, u32[]{:S(2)}) copy-start(f32[128,64]{0,1:T(8,128)S(1)} %get-tuple-element.323) | copy-start | bytes 98308
  77.1 361.2 %all-gather.23.cloned.1.call-start = ((), (), s32[]{:S(2)}) async-start(), calls=%async_computation.10 | async-start | bytes 10485760 | tf_op jit(solution)/shard_map/all_gather | solution.py:167
  77.7 398.1 %all-gather.17.cloned.1.call-start = ((), (), s32[]{:S(2)}) async-start(), calls=%async_computation.7 | async-start | bytes 1310720 | tf_op jit(solution)/shard_map/all_gather | solution.py:189
  123.4 509.2 %all-gather.25.cloned.1.call-start = ((), (), s32[]{:S(2)}) async-start(), calls=%async_computation.11 | async-start | bytes 10485760 | tf_op jit(solution)/shard_map/all_gather | solution.py:170
  123.9 779.7 %all-gather.29.cloned.1.call-start = ((), (), s32[]{:S(2)}) async-start(), calls=%async_computation.13 | async-start | bytes 31457280 | tf_op jit(solution)/shard_map/all_gather | solution.py:205
  124.7 1008.4 %all-gather.27.cloned.1.call-start = ((), (), s32[]{:S(2)}) async-start(), calls=%async_computation.12 | async-start | bytes 31457280 | tf_op jit(solution)/shard_map/all_gather | solution.py:203
  125.5 1237.1 %all-gather.31.cloned.1.call-start = ((), (), s32[]{:S(2)}) async-start(), calls=%async_computation.14 | async-start | bytes 31457280 | tf_op jit(solution)/shard_map/all_gather | solution.py:216
  126.2 1383.8 %reduce-scatter.7.cloned.1.call-start = ((), (), s32[]{:S(2)}) async-start(), calls=%async_computation.19 | async-start | bytes 1310720
  126.2 140.4 %collective-permute-start = (bf16[512,6144]{1,0:T(8,128)(2,1)}, bf16[512,6144]{1,0:T(8,128)(2,1)}, u32[]{:S(2)}, u32[]{:S(2)}) collective-permute-start(bf16[512,6144]{1,0:T(8,128)(2,1)} %param.29), channel_id=1, source_target_pairs={{0,24},{8,0},{16,8},{24,16},{1,25},{9,1},{17,9},{25,17},{2,26},{10... | collective-permute-start | bytes 18874376 | tf_op jit(solution)/shard_map/ppermute | solution.py:22
  129.1 149.5 %slice-start = ((s8[6291456]{0:T(1024)(128)(4,1)}), s8[4194304]{0:T(1024)(128)(4,1)S(1)}, s32[]{:S(2)}) async-start(s8[6291456]{0:T(1024)(128)(4,1)} %bitcast.322), calls=%async_computation.22 | async-start | bytes 8388608
  130.0 148.6 %slice-start.1 = ((s8[6291456]{0:T(1024)(128)(4,1)}), s8[2097152]{0:T(1024)(128)(4,1)S(1)}, s32[]{:S(2)}) async-start(s8[6291456]{0:T(1024)(128)(4,1)} %bitcast.322), calls=%async_computation.23 | async-start | bytes 4194304
  277.1 458.7 %collective-permute-start.1 = (bf16[1024,6144]{1,0:T(8,128)(2,1)}, bf16[1024,6144]{1,0:T(8,128)(2,1)}, u32[]{:S(2)}, u32[]{:S(2)}) collective-permute-start(bf16[1024,6144]{1,0:T(8,128)(2,1)} %pad_maximum_fusion.1), channel_id=1, source_target_pairs={{0,16},{8,24},{16,0},{24,8},{1,17},{9,25},{17,1},{25,9},{2,18},{10... | collective-permute-start | bytes 37748744 | tf_op jit(solution)/shard_map/ppermute | solution.py:22
  456.4 19.3 copy-start.28
  504.2 128.4 %copy-start.7 = (bf16[8,512,128]{2,1,0:T(8,128)(2,1)}, bf16[8,512,128]{2,1,0:T(8,128)(2,1)S(1)}, u32[]{:S(2)}) copy-start(bf16[8,512,128]{2,1,0:T(8,128)(2,1)S(1)} %get-tuple-element.621) | copy-start | bytes 3145732
  504.2 128.4 %copy-start.14 = (bf16[8,128,2,128]{3,1,2,0:T(8,128)(2,1)}, bf16[8,128,2,128]{3,1,2,0:T(8,128)(2,1)S(1)}, u32[]{:S(2)}) copy-start(bf16[8,128,2,128]{3,1,2,0:T(8,128)(2,1)S(1)} %get-tuple-element.633) | copy-start | bytes 1572868
  637.5 740.7 %copy-start.33 = (f32[128]{0:T(128)}, f32[128]{0:T(128)S(1)}, u32[]{:S(2)}) copy-start(f32[128]{0:T(128)S(1)} %add_rsqrt_fusion.2) | copy-start | bytes 1540
  637.5 109.1 %slice-start.2 = ((s8[6291456]{0:T(1024)(128)(4,1)}), s8[4194304]{0:T(1024)(128)(4,1)S(1)}, s32[]{:S(2)}) async-start(s8[6291456]{0:T(1024)(128)(4,1)} %bitcast.324), calls=%async_computation.24 | async-start | bytes 8388608
  638.5 108.1 %slice-start.3 = ((s8[6291456]{0:T(1024)(128)(4,1)}), s8[2097152]{0:T(1024)(128)(4,1)S(1)}, s32[]{:S(2)}) async-start(s8[6291456]{0:T(1024)(128)(4,1)} %bitcast.324), calls=%async_computation.25 | async-start | bytes 4194304
  756.0 147.7 %copy-start.4 = (bf16[1,128,2048]{2,1,0:T(8,128)(2,1)S(1)}, bf16[1,128,2048]{2,1,0:T(8,128)(2,1)}, u32[]{:S(2)}) copy-start(bf16[1,128,2048]{2,1,0:T(8,128)(2,1)} %param.31) | copy-start | bytes 1572868
  1133.1 13.9 copy-start.11
  1481.9 59.5 %reduce-scatter.9.cloned.1.call-start = ((), (), s32[]{:S(2)}) async-start(), calls=%async_computation.20 | async-start | bytes 1310720
  1486.8 55.9 %copy-start.9 = (f32[128,8,128]{0,2,1:T(8,128)S(1)}, f32[128,8,128]{0,2,1:T(8,128)}, u32[]{:S(2)}) copy-start(f32[128,8,128]{0,2,1:T(8,128)} %copy-done.8) | copy-start | bytes 1572868
  1486.8 55.9 %copy-start.36 = (f32[128]{0:T(128)S(1)}, f32[128]{0:T(128)}, u32[]{:S(2)}) copy-start(f32[128]{0:T(128)} %param.25) | copy-start | bytes 1540
  1486.8 116.5 %all-gather.39.cloned.1.call-start = ((), (), s32[]{:S(2)}) async-start(), calls=%async_computation.18 | async-start | bytes 2621440 | tf_op jit(solution)/shard_map/all_gather | solution.py:282
  1487.4 149.4 %all-gather.37.cloned.1.call-start = ((), (), s32[]{:S(2)}) async-start(), calls=%async_computation.17 | async-start | bytes 2621440 | tf_op jit(solution)/shard_map/all_gather | solution.py:281
  1488.2 205.9 %all-gather.33.cloned.1.call-start = ((), (), s32[]{:S(2)}) async-start(), calls=%async_computation.15 | async-start | bytes 5242880 | tf_op jit(solution)/shard_map/all_gather | solution.py:279
  1491.1 52.6 %copy-start.13 = (bf16[128,16,128]{0,2,1:T(8,128)(2,1)S(1)}, bf16[128,16,128]{0,2,1:T(8,128)(2,1)}, u32[]{:S(2)}) copy-start(bf16[128,16,128]{0,2,1:T(8,128)(2,1)} %multiply_convert_fusion.4) | copy-start | bytes 1572868
  1544.9 273.9 %all-gather.35.cloned.1.call-start = ((), (), s32[]{:S(2)}) async-start(), calls=%async_computation.16 | async-start | bytes 15728640 | tf_op jit(solution)/shard_map/all_gather | solution.py:280
  1548.7 21.9 copy-start.32
  1548.7 24.3 %copy-start.12 = (bf16[128,2048]{1,0:T(8,128)(2,1)S(1)}, bf16[128,2048]{1,0:T(8,128)(2,1)}, u32[]{:S(2)}) copy-start(bf16[128,2048]{1,0:T(8,128)(2,1)} %multiply_convert_fusion.5) | copy-start | bytes 1572868
  1548.8 15.8 all-to-all-start.2
  1564.5 35.1 %all-to-all-start.3 = ((bf16[128,4,1536]{2,0,1:T(8,128)(2,1)}), bf16[128,4,1536]{2,0,1:T(8,128)(2,1)}, u32[]{:S(2)}, u32[]{:S(2)}) async-start(bf16[128,4,1536]{2,0,1:T(8,128)(2,1)} %bitcast.331), calls=%async_computation.3 | async-start | bytes 3145728 | tf_op jit(solution)/shard_map/all_to_all | solution.py:277
  1599.6 41.4 %all-to-all-start = ((bf16[128,4,512]{2,0,1:T(8,128)(2,1)}), bf16[128,4,512]{2,0,1:T(8,128)(2,1)S(1)}, u32[]{:S(2)}, u32[]{:S(2)}) async-start(bf16[128,4,512]{2,0,1:T(8,128)(2,1)} %fusion.58), calls=%async_computation | async-start | bytes 1048576 | tf_op jit(solution)/shard_map/all_to_all | solution.py:274
  1641.0 59.7 %all-to-all-start.1 = ((bf16[128,4,512]{2,0,1:T(8,128)(2,1)}), bf16[128,4,512]{2,0,1:T(8,128)(2,1)S(1)}, u32[]{:S(2)}, u32[]{:S(2)}) async-start(bf16[128,4,512]{2,0,1:T(8,128)(2,1)} %bitcast.257), calls=%async_computation.1 | async-start | bytes 1048576 | tf_op jit(solution)/shard_map/all_to_all | solution.py:275
  1644.5 686.7 %all-reduce.4.cloned.1.call-start = ((), (), s32[]{:S(2)}) async-start(), calls=%async_computation.21 | async-start | bytes 50331648 | tf_op jit(solution)/shard_map/psum | solution.py:289
  1857.2 46.8 %copy-start.5 = (bf16[1,128,2048]{2,1,0:T(8,128)(2,1)S(1)}, bf16[1,128,2048]{2,1,0:T(8,128)(2,1)}, u32[]{:S(2)}) copy-start(bf16[1,128,2048]{2,1,0:T(8,128)(2,1)} %param.31) | copy-start | bytes 1572868
  1857.2 46.8 %copy-start.6 = (f32[128,2048]{1,0:T(8,128)S(1)}, f32[128,2048]{1,0:T(8,128)}, u32[]{:S(2)}) copy-start(f32[128,2048]{1,0:T(8,128)} %get-tuple-element.330) | copy-start | bytes 3145732
  1857.2 46.8 %copy-start.27 = (f32[2048]{0:T(1024)S(1)}, f32[2048]{0:T(1024)}, u32[]{:S(2)}) copy-start(f32[2048]{0:T(1024)} %param.27) | copy-start | bytes 24580
  1857.3 46.8 %copy-start.34 = (f32[128]{0:T(128)S(1)}, f32[128]{0:T(128)}, u32[]{:S(2)}) copy-start(f32[128]{0:T(128)} %copy-done.33) | copy-start | bytes 1540
  1857.3 46.8 %copy-start.40 = (f32[128]{0:T(128)S(1)}, f32[128]{0:T(128)}, u32[]{:S(2)}) copy-start(f32[128]{0:T(128)} %copy-done.39) | copy-start | bytes 1540
  2331.2 18.0 copy-start
  (21 other events, 137.2 us)
Sparse Core Ops, SparseCore 0:
  9.9 55.2 all-gather.18
  67.0 52.5 all-gather.14
  122.0 160.2 all-gather.20
  284.0 154.2 all-gather.22
  440.6 35.1 all-gather.16
  477.4 155.0 all-gather.24
  634.4 269.1 all-gather.28
  905.5 227.5 all-gather.26
  1135.0 227.5 all-gather.30
  1482.0 27.9 reduce-scatter.6
  1513.4 27.9 reduce-scatter.8
  1543.1 56.6 all-gather.38
  1601.7 35.1 all-gather.36
  1639.1 54.9 all-gather.32
  1696.4 122.3 all-gather.34
  1839.6 491.5 all-reduce.3
